TPU v7x, 32 devices: a whole 2x2x4 slice. The times are simulated.
32 devices in a mesh: row: 4 (over x, core), col: 8 (over z, y).
Axes of the slice: x: 2, y: 2, z: 4, core: 2. Of those that a mesh axis runs over, the one named last changes fastest.
Arguments:
- hamiltonian: bfloat16 [2912, 2912], P('row', 'col'), may hold values from -6 to 6
- new_atom: int32 [224], replicated, may hold values from 0 to 223, as said below
- pattern: int32 [224, 224], P('row', 'col'), may hold values 0 or 1
Outputs:
- sign_matrix: float32 [2912, 2912], P('row', 'col')
Inputs may be any that keep to these rules, and one draw needn't show every extreme that they name: `new_atom`: each old atom appears once. Block column b holds atoms b * 28 to (b + 1) * 28 - 1 in both orders. For each new block column d and each v from 0 to 27, exactly one atom of new block column d comes from old block column (d - 1 - (v mod 8)) mod 8, so the number of atoms that old block column b sends to new block column (b + k) mod 8 is the number of such v with (1 + v) mod 8 = k.
All inputs are finite; a program needn't handle non-finite values. No bound on the sum of `pattern` on one device may be relied on, other than what follows from the above.
Results may differ from a plain program's by a relative error of at most 0.0029.
Values may be sent and summed in bfloat16 or wider, within the bound.
A program may use at most 64 MiB of HBM per device.

v0:
```python
import jax
import jax.numpy as jnp
import numpy as np
from jax import lax
from jax.sharding import PartitionSpec as P

NBF = 13


def expand(atoms):
    return (atoms[:, None] * NBF + jnp.arange(NBF, dtype=jnp.int32)[None, :]).reshape(-1)


def pack_slots(new_atom, here, per_block, groups, slots):
    source = new_atom.reshape(groups, per_block) // per_block
    local = new_atom.reshape(groups, per_block) - here * per_block
    mine = source == here
    rank = jnp.cumsum(mine.astype(jnp.int32), axis=1) - 1
    number = jnp.arange(slots, dtype=jnp.int32)
    hit = mine[:, None, :] & (rank[:, None, :] == number[None, :, None])
    atoms = jnp.sum(jnp.where(hit, local[:, None, :], 0), axis=2)
    used = jnp.any(hit, axis=2)
    return (atoms.reshape(-1), jnp.repeat(used.reshape(-1), NBF))


def place_slots(new_atom, here, per_block, groups, slots):
    source = lax.dynamic_slice_in_dim(new_atom, here * per_block, per_block) // per_block
    onehot = source[:, None] == jnp.arange(groups, dtype=jnp.int32)[None, :]
    running = jnp.cumsum(onehot.astype(jnp.int32), axis=0) - 1
    rank = jnp.sum(jnp.where(onehot, running, 0), axis=1)
    return expand((source * slots + rank).astype(jnp.int32))


def fold_right(row_panel, right):
    return jnp.dot(
        row_panel,
        lax.all_gather(right, "row", axis=0, tiled=True),
        preferred_element_type=jnp.float32,
    )


def on_device(hamiltonian, new_atom, pattern):
    rows_here, cols_here = hamiltonian.shape
    row_count = lax.axis_size("row")
    col_count = lax.axis_size("col")
    order_all = rows_here * row_count
    atoms_row = rows_here // NBF
    atoms_col = cols_here // NBF
    ratio = col_count // row_count
    counts = np.bincount((1 + np.arange(atoms_col)) % col_count, minlength=col_count)
    targets = (np.arange(ratio)[:, None] + np.arange(col_count)[None, :]) % col_count // ratio
    per_target = np.sum(
        (targets[None, :, :] == np.arange(row_count)[:, None, None]) * counts[None, None, :],
        axis=(1, 2),
    )
    slots_row = max(int(np.max(per_target)), 1)
    slots_col = max(int(np.max(counts)), 1)
    row_here = lax.axis_index("row")
    col_here = lax.axis_index("col")
    atoms, flags = pack_slots(new_atom, row_here, atoms_row, row_count, slots_row)
    outgoing = jnp.where(
        flags[:, None], jnp.take(hamiltonian, expand(atoms), axis=0), jnp.zeros((), jnp.bfloat16)
    )
    arrived = lax.all_to_all(outgoing, "row", split_axis=0, concat_axis=0, tiled=True)
    moved = jnp.take(
        arrived, place_slots(new_atom, row_here, atoms_row, row_count, slots_row), axis=0
    )
    atoms, flags = pack_slots(new_atom, col_here, atoms_col, col_count, slots_col)
    outgoing = jnp.where(
        flags[None, :], jnp.take(moved, expand(atoms), axis=1), jnp.zeros((), jnp.bfloat16)
    )
    arrived = lax.all_to_all(outgoing, "col", split_axis=1, concat_axis=1, tiled=True)
    moved = jnp.take(
        arrived, place_slots(new_atom, col_here, atoms_col, col_count, slots_col), axis=1
    )
    atom_rows, atom_cols = pattern.shape
    keep = jnp.broadcast_to(
        pattern.astype(jnp.float32)[:, None, :, None], (atom_rows, NBF, atom_cols, NBF)
    ).reshape(rows_here, cols_here)
    masked = moved.astype(jnp.float32) * keep
    total = lax.psum(jnp.sum(masked * masked), ("row", "col"))
    start = (masked * lax.rsqrt(total / order_all)).astype(jnp.bfloat16)
    first = lax.all_gather(start, "col", axis=1, tiled=True)
    square = (fold_right(first, start) * keep).astype(jnp.bfloat16)
    second = lax.all_gather(start, "col", axis=1, tiled=True)
    cube = fold_right(second, square) * keep
    return keep * (1.5 * start.astype(jnp.float32) - 0.5 * cube)


def solution(mesh):
    in_specs = (P("row", "col"), P(), P("row", "col"))
    out_specs = P("row", "col")
    return jax.shard_map(
        on_device, mesh=mesh, in_specs=in_specs, out_specs=out_specs, check_vma=False
    )
```

profile of v0, /device:TPU:0, one launch (start us, length us, event | category | flops | bytes accessed | tf_op | source)
XLA Modules:
  0.0 246.0 jit_solution(5118682109715307969)
XLA Ops:
  6.5 0.8 compare_and_fusion.5
  7.3 0.7 broadcast_divide_fusion.1
  8.0 0.1 sub.80
  8.1 0.1 and.101
  8.2 0.1 div.54
  8.3 0.2 reduce_window_sum.47
  8.5 0.2 fusion.9
  8.6 0.2 select_reduce_fusion
  8.8 0.1 mul.113
  9.0 0.2 add.307
  9.2 0.1 add.298
  9.3 0.1 add.300
  9.5 0.1 broadcast_in_dim.144
  9.6 3.5 %gather_fusion = bf16[832,364]{1,0:T(8,128)(2,1)S(1)} fusion(bf16[728,364]{1,0:T(8,128)(2,1)S(1)} %copy-done, s32[1024]{0:T(1024)S(1)} %pad_clamp_fusion.3), kind=kCustom, calls=%fused_computation | custom fusion | bytes 1214720 | tf_op jit(solution)/shard_map/jit(_take)/gather | solution.py:62
  13.2 1.1 select_select_fusion.1
  14.3 4.2 %all-to-all-start = ((bf16[4,208,364]{2,1,0:T(8,128)(2,1)}), bf16[4,208,364]{2,1,0:T(8,128)(2,1)S(1)}, u32[]{:S(2)}, u32[]{:S(2)}) async-start(bf16[4,208,364]{2,1,0:T(8,128)(2,1)} %select_select_fusion.1), calls=%async_computation | async-start | bytes 1277952 | tf_op jit(solution)/shard_map/all_to_all | solution.py:64
  18.5 0.1 and_select_fusion
  18.7 0.1 reduce_window_sum.46
  18.8 0.2 select_reduce_fusion.1
  19.0 0.1 add_multiply_fusion
  19.1 0.1 add.310
  19.4 0.1 and.94
  19.6 0.2 reduce_window_sum.45
  19.8 0.1 fusion.13
  19.9 0.2 select_reduce_fusion.2
  20.1 0.1 copy.26
  20.3 0.1 add.316
  20.5 0.1 and_select_fusion.1
  20.5 0.1 add.294
  20.7 0.1 add.283
  20.9 0.1 copy.25
  21.1 0.1 broadcast_in_dim.136
  21.2 7.4 %all-to-all-done = bf16[4,208,364]{2,1,0:T(8,128)(2,1)S(1)} async-done(((bf16[4,208,364]{2,1,0:T(8,128)(2,1)}), bf16[4,208,364]{2,1,0:T(8,128)(2,1)S(1)}, u32[]{:S(2)}, u32[]{:S(2)}) %all-to-all-start) | async-done | bytes 605728 | tf_op jit(solution)/shard_map/all_to_all | solution.py:64
  28.6 3.0 %gather_fusion.1 = bf16[728,364]{1,0:T(8,128)(2,1)S(1)} fusion(bf16[832,364]{1,0:T(8,128)(2,1)S(1)} %bitcast.33, s32[1024]{0:T(1024)S(1)} %pad_clamp_fusion.2), kind=kCustom, calls=%fused_computation.1 | custom fusion | bytes 1062880 | tf_op jit(solution)/shard_map/jit(_take)/gather | solution.py:65
  31.5 0.2 broadcast_select_fusion
  31.7 0.2 copy.28
  32.0 2.2 gather_fusion.2
  34.1 0.1 gather.24
  34.3 1.0 select_select_fusion
  35.3 6.5 %all-to-all-start.1 = ((bf16[728,8,52]{0,2,1:T(8,128)(2,1)}), bf16[728,8,52]{0,2,1:T(8,128)(2,1)S(1)}, u32[]{:S(2)}, u32[]{:S(2)}) async-start(bf16[728,8,52]{0,2,1:T(8,128)(2,1)} %select_select_fusion), calls=%async_computation.1 | async-start | bytes 1376256 | tf_op jit(solution)/shard_map/all_to_all | solution.py:72
  42.0 0.2 select_reduce_fusion.3
  42.2 0.1 add_multiply_fusion.1
  42.4 0.1 add.319
  42.5 0.1 add.279
  42.6 4.7 %broadcast_in_dim.132 = f32[56,13,28,13]{1,0,3,2:T(8,128)} broadcast(f32[56,28]{0,1:T(8,128)S(1)} %convert_element_type.41), dimensions={0,2} | broadcast | bytes 1066240 | tf_op jit(solution)/shard_map/broadcast_in_dim | solution.py:77
  47.3 6.7 %reshape.368 = f32[728,364]{0,1:T(8,128)S(1)} reshape(f32[56,13,28,13]{1,0,3,2:T(8,128)} %broadcast_in_dim.132) | data formatting | bytes 2119936 | tf_op jit(solution)/shard_map/reshape | solution.py:79
  54.1 0.4 copy.36
  54.5 0.1 broadcast_in_dim.154
  54.7 4.9 %all-to-all-done.1 = bf16[728,8,52]{0,2,1:T(8,128)(2,1)S(1)} async-done(((bf16[728,8,52]{0,2,1:T(8,128)(2,1)}), bf16[728,8,52]{0,2,1:T(8,128)(2,1)S(1)}, u32[]{:S(2)}, u32[]{:S(2)}) %all-to-all-start.1) | async-done | bytes 605728 | tf_op jit(solution)/shard_map/all_to_all | solution.py:72
  59.6 0.3 all_to_all.15
  59.8 2.2 gather_fusion.3
  62.0 0.3 copy.29
  62.3 0.9 fusion.5
  63.2 38.4 %psum.7 = f32[]{:T(128)} all-reduce(f32[]{:T(128)} %fusion.5), channel_id=1, replica_groups=mesh['row'=4,'col'=8] {'row','col'}, use_global_device_ids=true, to_apply=%region_11.12 | all-reduce | flops 1 | bytes 8 | tf_op jit(solution)/shard_map/psum | solution.py:81
  102.3 1.0 fusion.7
  103.3 0.7 all-gather.5.cloned.1.call-update
  104.1 0.2 all-gather.7.cloned.1.call-start
  104.3 75.6 %all-gather.9.cloned.1.call-done = bf16[8,364,728]{1,2,0:T(8,128)(2,1)} async-done(((bf16[1,364,728]{1,2,0:T(8,128)(2,1)}), bf16[8,364,728]{1,2,0:T(8,128)(2,1)}) %all-gather.9.cloned.1.call-update) | async-done | bytes 4239888 | tf_op jit(solution)/shard_map/all_gather | solution.py:85
  179.9 4.9 %copy.33 = bf16[8,364,728]{1,0,2:T(8,128)(2,1)} copy(bf16[8,364,728]{1,2,0:T(8,128)(2,1)} %all-gather.9.cloned.1.call-done) | data formatting | bytes 8479744 | tf_op jit(solution)/shard_map/all_gather | solution.py:85
  184.8 8.7 %reshape.402 = bf16[2912,728]{0,1:T(8,128)(2,1)} reshape(bf16[8,364,728]{1,0,2:T(8,128)(2,1)} %copy.33) | data formatting | bytes 8479744
  193.5 9.8 %all-gather.5.cloned.1.call-done = bf16[2912,364]{1,0:T(8,128)(2,1)} async-done(((bf16[728,364]{1,0:T(8,128)(2,1)}), bf16[2912,364]{1,0:T(8,128)(2,1)}) %all-gather.5.cloned.1.call-update) | async-done | bytes 2119952 | tf_op jit(solution)/shard_map/all_gather | solution.py:37
  203.3 6.2 %fusion.3 = bf16[728,364]{1,0:T(8,128)(2,1)} fusion(f32[728,364]{1,0:T(8,128)S(1)} %copy.36, bf16[2912,728]{0,1:T(8,128)(2,1)} %reshape.402, bf16[2912,364]{1,0:T(8,128)(2,1)} %all-gather.5.cloned.1.call-done), kind=kOutput, calls=%fused_computation.9 | convolution fusion | flops 1543843328 | bytes 7949760 | tf_op jit(solution)/shard_map/dot_general | solution.py:35
  209.5 23.5 %all-gather.7.cloned.1.call-done = bf16[2912,364]{1,0:T(8,128)(2,1)} async-done(((bf16[728,364]{1,0:T(8,128)(2,1)}), bf16[2912,364]{1,0:T(8,128)(2,1)}) %all-gather.7.cloned.1.call-update) | async-done | bytes 2119952 | tf_op jit(solution)/shard_map/all_gather | solution.py:37
  233.0 6.4 %fusion.2 = f32[728,364]{1,0:T(8,128)} fusion(f32[728,364]{1,0:T(8,128)S(1)} %copy.36, bf16[2912,728]{0,1:T(8,128)(2,1)} %reshape.402, bf16[2912,364]{1,0:T(8,128)(2,1)} %all-gather.7.cloned.1.call-done, bf16[728,364]{1,0:T(8,128)(2,1)S(1)} %copy-done.1), kind=kOutput, calls=%fused_computation.8 | convolution fusion | flops 1544903168 | bytes 9009728 | tf_op jit(solution)/shard_map/dot_general | solution.py:35
  (49 shorter events, 1.5 us)
Async XLA Ops:
  6.5 3.1 %copy-start = (bf16[728,364]{1,0:T(8,128)(2,1)S(1)}, bf16[728,364]{1,0:T(8,128)(2,1)}, u32[]{:S(2)}) copy-start(bf16[728,364]{1,0:T(8,128)(2,1)} %param.3) | copy-start | bytes 1589956
  13.1 5.4 %copy-start.3 = (s32[224]{0:T(256)S(1)}, s32[224]{0:T(256)}, u32[]{:S(2)}) copy-start(s32[224]{0:T(256)} %param.4) | copy-start | bytes 2692
  14.3 14.3 %all-to-all-start = ((bf16[4,208,364]{2,1,0:T(8,128)(2,1)}), bf16[4,208,364]{2,1,0:T(8,128)(2,1)S(1)}, u32[]{:S(2)}, u32[]{:S(2)}) async-start(bf16[4,208,364]{2,1,0:T(8,128)(2,1)} %select_select_fusion.1), calls=%async_computation | async-start | bytes 1277952 | tf_op jit(solution)/shard_map/all_to_all | solution.py:64
  34.3 8.3 %copy-start.2 = (s32[56,28]{0,1:T(8,128)S(1)}, s32[56,28]{0,1:T(8,128)}, u32[]{:S(2)}) copy-start(s32[56,28]{0,1:T(8,128)} %param.5) | copy-start | bytes 18820
  35.3 24.2 %all-to-all-start.1 = ((bf16[728,8,52]{0,2,1:T(8,128)(2,1)}), bf16[728,8,52]{0,2,1:T(8,128)(2,1)S(1)}, u32[]{:S(2)}, u32[]{:S(2)}) async-start(bf16[728,8,52]{0,2,1:T(8,128)(2,1)} %select_select_fusion), calls=%async_computation.1 | async-start | bytes 1376256 | tf_op jit(solution)/shard_map/all_to_all | solution.py:72
  41.9 138.0 %all-gather.9.cloned.1.call-start = ((), (), s32[]{:S(2)}) async-start(), calls=%async_computation.4 | async-start | bytes 5031936 | tf_op jit(solution)/shard_map/all_gather | solution.py:85
  103.3 100.0 %all-gather.5.cloned.1.call-start = ((), (), s32[]{:S(2)}) async-start(), calls=%async_computation.2 | async-start | bytes 2795520 | tf_op jit(solution)/shard_map/all_gather | solution.py:37
  104.1 129.0 %all-gather.7.cloned.1.call-start = ((), (), s32[]{:S(2)}) async-start(), calls=%async_computation.3 | async-start | bytes 2795520 | tf_op jit(solution)/shard_map/all_gather | solution.py:37
  193.5 39.5 %copy-start.1 = (bf16[728,364]{1,0:T(8,128)(2,1)S(1)}, bf16[728,364]{1,0:T(8,128)(2,1)}, u32[]{:S(2)}) copy-start(bf16[728,364]{1,0:T(8,128)(2,1)} %fusion.7) | copy-start | bytes 1589956
Sparse Core Ops, SparseCore 0:
  103.4 76.4 all-gather.8
  181.4 21.7 all-gather.4
  209.7 23.3 all-gather.6
where the time goes:
time: 247 us; the launch traced here: 246 us
  waiting for transfers between devices  122 us (49%)
  local copies, waits for them, and re-layouts  39.7 us (16%)
  blocking collectives  38.4 us (16%)
  between operations  14.1 us (6%)
  matrix products  12.7 us (5%)
  starting transfers between devices  11.1 us (4%)
  other arithmetic  8.25 us (3%)
    all_gather x1, waiting for transfers between devices, on_device(): second = lax.all_gather(start, 'col', axis=1, tiled=True)  75.6 us
    psum x1, blocking collectives, on_device(): total = lax.psum(jnp.sum(masked * masked), ('row', 'col'))  38.4 us
    all_gather x2, waiting for transfers between devices, fold_right(): lax.all_gather(right, 'row', axis=0, tiled=True)  33.3 us
    dot_general x2, matrix products, fold_right(): jnp.dot(row_panel, lax.all_gather(right, 'row', axis=0, tiled=True), pref...  12.7 us
    unnamed x9, local copies, waits for them, and re-layouts  8.69 us
    all_to_all x1, waiting for transfers between devices, on_device(): lax.all_to_all(outgoing, 'row', split_axis=0, concat_axis=0, tiled=True)  7.35 us
    reshape x2, local copies, waits for them, and re-layouts, on_device(): keep = jnp.broadcast_to(pattern.astype(jnp.float32)[:, None, :, None], (a...  7.1 us
    all_to_all x1, starting transfers between devices, on_device(): lax.all_to_all(outgoing, 'col', split_axis=1, concat_axis=1, tiled=True)  6.53 us
  transfers between devices with their start and end apart: 5, of which 5 were waited for; matrix products, arithmetic and copies ran while one was open for 12% of the time, Pallas kernels for 0%

commit v1 on v0

--- a/solution.py
+++ b/solution.py
@@ -82,7 +82,8 @@
     start = (masked * lax.rsqrt(total / order_all)).astype(jnp.bfloat16)
     first = lax.all_gather(start, "col", axis=1, tiled=True)
     square = (fold_right(first, start) * keep).astype(jnp.bfloat16)
-    second = lax.all_gather(start, "col", axis=1, tiled=True)
+    pieces = lax.all_gather(start, "col")
+    second = jnp.concatenate(pieces, axis=1)
     cube = fold_right(second, square) * keep
     return keep * (1.5 * start.astype(jnp.float32) - 0.5 * cube)
 

time: 247 us -> 319 us (1.29)
  waiting for transfers between devices: 122 us -> 170 us
  local copies, waits for them, and re-layouts: 39.7 us -> 61.5 us
    all_gather x1 -> x2, waiting for transfers between devices: 75.6 us -> 137 us  [the longest x1 72.3 us: on_device(): pieces = lax.all_gather(start, 'col')]
    all_gather x2, waiting for transfers between devices: 33.3 us -> 19.3 us  [fold_right(): lax.all_gather(right, 'row', axis=0, tiled=True)]
    reshape x0 -> x2, local copies, waits for them, and re-layouts: none -> 13.7 us  [on_device(): second = jnp.concatenate(pieces, axis=1)]
    reshape x2 -> x4, local copies, waits for them, and re-layouts: 7.1 us -> 15.2 us  [on_device(): keep = jnp.broadcast_to(pattern.astype(jnp.float32)[:, None, :, None], (a...]
  transfers between devices with their start and end apart: 5 -> 6, of which waited for: 5 -> 6; matrix products, arithmetic and copies ran while one was open for 12% -> 19% of each run, Pallas kernels for 0% -> 0%
where the time goes in v1:
time: 319 us; the launch traced here: 318 us
  waiting for transfers between devices  170 us (53%)
  local copies, waits for them, and re-layouts  61.5 us (19%)
  blocking collectives  38.4 us (12%)
  between operations  14.1 us (4%)
  matrix products  12.7 us (4%)
  starting transfers between devices  11.1 us (3%)
  other arithmetic  10.6 us (3%)
    all_gather x1, waiting for transfers between devices, on_device(): pieces = lax.all_gather(start, 'col')  72.3 us
    all_gather x1, waiting for transfers between devices, on_device(): first = lax.all_gather(start, 'col', axis=1, tiled=True)  65 us
    psum x1, blocking collectives, on_device(): total = lax.psum(jnp.sum(masked * masked), ('row', 'col'))  38.4 us
    all_gather x2, waiting for transfers between devices, fold_right(): lax.all_gather(right, 'row', axis=0, tiled=True)  19.3 us
    reshape x4, local copies, waits for them, and re-layouts, on_device(): keep = jnp.broadcast_to(pattern.astype(jnp.float32)[:, None, :, None], (a...  15.2 us
    reshape x2, local copies, waits for them, and re-layouts, on_device(): second = jnp.concatenate(pieces, axis=1)  13.7 us
    dot_general x2, matrix products, fold_right(): jnp.dot(row_panel, lax.all_gather(right, 'row', axis=0, tiled=True), pref...  12.7 us
    unnamed x9, local copies, waits for them, and re-layouts  8.7 us
  transfers between devices with their start and end apart: 6, of which 6 were waited for; matrix products, arithmetic and copies ran while one was open for 19% of the time, Pallas kernels for 0%

profile of v1, /device:TPU:0, one launch (start us, length us, event | category | flops | bytes accessed | tf_op | source)
XLA Modules:
  0.0 318.0 jit_solution(3479221268036356339)
XLA Ops:
  6.5 0.8 compare_and_fusion.5
  7.3 0.1 and.101
  7.4 0.7 broadcast_divide_fusion.1
  8.2 0.2 reduce_window_sum.47
  8.5 0.1 fusion.5
  8.6 0.2 select_reduce_fusion
  9.0 0.1 broadcast_in_dim.148
  9.1 0.1 add.298
  9.3 0.1 add.307
  9.5 0.1 add.300
  9.6 3.5 %gather_fusion = bf16[832,364]{1,0:T(8,128)(2,1)S(1)} fusion(bf16[728,364]{1,0:T(8,128)(2,1)S(1)} %copy-done, s32[1024]{0:T(1024)S(1)} %pad_clamp_fusion.3), kind=kCustom, calls=%fused_computation | custom fusion | bytes 1214720 | tf_op jit(solution)/shard_map/jit(_take)/gather | solution.py:62
  13.1 1.1 select_select_fusion.1
  14.3 4.2 %all-to-all-start = ((bf16[4,208,364]{2,1,0:T(8,128)(2,1)}), bf16[4,208,364]{2,1,0:T(8,128)(2,1)S(1)}, u32[]{:S(2)}, u32[]{:S(2)}) async-start(bf16[4,208,364]{2,1,0:T(8,128)(2,1)} %select_select_fusion.1), calls=%async_computation | async-start | bytes 1277952 | tf_op jit(solution)/shard_map/all_to_all | solution.py:64
  18.6 0.1 and.94
  18.8 0.2 reduce_window_sum.45
  19.0 0.1 fusion.9
  19.2 0.2 select_reduce_fusion.2
  19.6 0.1 add.316
  19.8 0.1 reduce_window_sum.46
  19.9 0.2 select_reduce_fusion.1
  20.1 0.1 add_multiply_fusion
  20.3 0.1 add.310
  20.4 0.1 and_select_fusion.1
  20.5 0.1 add.294
  20.7 0.1 copy.26
  20.8 0.1 broadcast_in_dim.140
  21.2 7.4 %all-to-all-done = bf16[4,208,364]{2,1,0:T(8,128)(2,1)S(1)} async-done(((bf16[4,208,364]{2,1,0:T(8,128)(2,1)}), bf16[4,208,364]{2,1,0:T(8,128)(2,1)S(1)}, u32[]{:S(2)}, u32[]{:S(2)}) %all-to-all-start) | async-done | bytes 605728 | tf_op jit(solution)/shard_map/all_to_all | solution.py:64
  28.6 3.0 gather_fusion.1
  31.5 0.2 broadcast_select_fusion
  31.7 0.2 copy.29
  31.9 2.2 gather_fusion.2
  34.1 0.1 gather.26
  34.3 1.0 select_select_fusion
  35.3 6.5 %all-to-all-start.1 = ((bf16[728,8,52]{0,2,1:T(8,128)(2,1)}), bf16[728,8,52]{0,2,1:T(8,128)(2,1)S(1)}, u32[]{:S(2)}, u32[]{:S(2)}) async-start(bf16[728,8,52]{0,2,1:T(8,128)(2,1)} %select_select_fusion), calls=%async_computation.1 | async-start | bytes 1376256 | tf_op jit(solution)/shard_map/all_to_all | solution.py:72
  42.0 0.2 select_reduce_fusion.3
  42.2 0.1 add_multiply_fusion.1
  42.4 0.1 add.319
  42.5 0.1 add.279
  42.7 0.1 broadcast_in_dim.158
  42.8 4.7 %broadcast_in_dim.136 = f32[56,13,28,13]{1,0,3,2:T(8,128)} broadcast(f32[56,28]{0,1:T(8,128)S(1)} %convert_element_type.59), dimensions={0,2} | broadcast | bytes 1066240 | tf_op jit(solution)/shard_map/broadcast_in_dim | solution.py:77
  47.5 6.7 %reshape.422 = f32[728,364]{0,1:T(8,128)S(1)} reshape(f32[56,13,28,13]{1,0,3,2:T(8,128)} %broadcast_in_dim.136) | data formatting | bytes 2119936 | tf_op jit(solution)/shard_map/reshape | solution.py:79
  54.3 0.4 copy.38
  54.7 4.9 %all-to-all-done.1 = bf16[728,8,52]{0,2,1:T(8,128)(2,1)S(1)} async-done(((bf16[728,8,52]{0,2,1:T(8,128)(2,1)}), bf16[728,8,52]{0,2,1:T(8,128)(2,1)S(1)}, u32[]{:S(2)}, u32[]{:S(2)}) %all-to-all-start.1) | async-done | bytes 605728 | tf_op jit(solution)/shard_map/all_to_all | solution.py:72
  59.6 0.3 all_to_all.15
  59.8 2.2 gather_fusion.3
  62.0 0.3 copy.30
  62.3 0.9 multiply_reduce_fusion
  63.2 38.4 %psum.7 = f32[]{:T(128)} all-reduce(f32[]{:T(128)} %multiply_reduce_fusion), channel_id=1, replica_groups=mesh['row'=4,'col'=8] {'row','col'}, use_global_device_ids=true, to_apply=%region_11.12 | all-reduce | flops 1 | bytes 8 | tf_op jit(solution)/shard_map/psum | solution.py:81
  102.3 1.0 multiply_convert_fusion.1
  103.4 0.7 all-gather.8.cloned.1.call-update
  104.1 6.8 %reshape.423 = f32[1,728,364]{1,2,0:T(8,128)S(1)} reshape(f32[56,13,28,13]{1,0,3,2:T(8,128)} %broadcast_in_dim.136) | data formatting | bytes 2119936 | tf_op jit(solution)/shard_map/reshape | solution.py:79
  110.9 1.4 copy.33
  112.2 2.4 multiply_convert_fusion
  114.6 0.2 all-gather.10.cloned.1.call-start
  114.9 65.0 %all-gather.12.cloned.1.call-done = bf16[8,364,728]{1,2,0:T(8,128)(2,1)} async-done(((bf16[1,364,728]{1,2,0:T(8,128)(2,1)}), bf16[8,364,728]{1,2,0:T(8,128)(2,1)}) %all-gather.12.cloned.1.call-update) | async-done | bytes 4239888 | tf_op jit(solution)/shard_map/all_gather | solution.py:83
  179.9 4.9 %copy.35 = bf16[8,364,728]{1,0,2:T(8,128)(2,1)} copy(bf16[8,364,728]{1,2,0:T(8,128)(2,1)} %all-gather.12.cloned.1.call-done) | data formatting | bytes 8479744 | tf_op jit(solution)/shard_map/all_gather | solution.py:83
  184.9 8.7 %reshape.459 = bf16[2912,728]{0,1:T(8,128)(2,1)} reshape(bf16[8,364,728]{1,0,2:T(8,128)(2,1)} %copy.35) | data formatting | bytes 8479744
  193.5 9.8 %all-gather.8.cloned.1.call-done = bf16[2912,364]{1,0:T(8,128)(2,1)} async-done(((bf16[728,364]{1,0:T(8,128)(2,1)}), bf16[2912,364]{1,0:T(8,128)(2,1)}) %all-gather.8.cloned.1.call-update) | async-done | bytes 2119952 | tf_op jit(solution)/shard_map/all_gather | solution.py:37
  203.3 6.2 %fusion.3 = bf16[728,364]{1,0:T(8,128)(2,1)} fusion(f32[728,364]{1,0:T(8,128)S(1)} %copy.38, bf16[2912,728]{0,1:T(8,128)(2,1)} %reshape.459, bf16[2912,364]{1,0:T(8,128)(2,1)} %all-gather.8.cloned.1.call-done), kind=kOutput, calls=%fused_computation.9 | convolution fusion | flops 1543843328 | bytes 7949760 | tf_op jit(solution)/shard_map/dot_general | solution.py:35
  209.5 72.3 %all-gather.6.cloned.1.call-done = bf16[8,728,364]{2,1,0:T(8,128)(2,1)} async-done(((bf16[1,728,364]{2,1,0:T(8,128)(2,1)}), bf16[8,728,364]{2,1,0:T(8,128)(2,1)}) %all-gather.6.cloned.1.call-update) | async-done | bytes 4239888 | tf_op jit(solution)/shard_map/all_gather | solution.py:85
  281.8 4.9 %copy.34 = bf16[728,8,364]{2,1,0:T(8,128)(2,1)} copy(bf16[728,8,364]{2,0,1:T(8,128)(2,1)} %bitcast.40) | data formatting | bytes 8479744 | tf_op jit(solution)/shard_map/reshape | solution.py:86
  286.7 8.7 %reshape.425 = bf16[728,2912]{1,0:T(8,128)(2,1)} reshape(bf16[728,8,364]{2,1,0:T(8,128)(2,1)} %copy.34) | data formatting | bytes 8479744 | tf_op jit(solution)/shard_map/reshape | solution.py:86
  295.5 9.5 %all-gather.10.cloned.1.call-done = bf16[2912,364]{1,0:T(8,128)(2,1)} async-done(((bf16[728,364]{1,0:T(8,128)(2,1)}), bf16[2912,364]{1,0:T(8,128)(2,1)}) %all-gather.10.cloned.1.call-update) | async-done | bytes 2119952 | tf_op jit(solution)/shard_map/all_gather | solution.py:37
  305.0 6.4 %fusion.2 = f32[728,364]{1,0:T(8,128)} fusion(f32[728,364]{1,0:T(8,128)S(1)} %copy.38, bf16[728,2912]{1,0:T(8,128)(2,1)} %reshape.425, bf16[2912,364]{1,0:T(8,128)(2,1)} %all-gather.10.cloned.1.call-done, bf16[728,364]{1,0:T(8,128)(2,1)S(1)} %copy-done.1), kind=kOutput, calls=%fused_computation.8 | convolution fusion | flops 1544903168 | bytes 9009728 | tf_op jit(solution)/shard_map/dot_general | solution.py:35
  (57 shorter events, 2.0 us)
Async XLA Ops:
  6.5 3.1 copy-start
  13.1 5.4 %copy-start.3 = (s32[224]{0:T(256)S(1)}, s32[224]{0:T(256)}, u32[]{:S(2)}) copy-start(s32[224]{0:T(256)} %param.4) | copy-start | bytes 2692
  14.3 14.3 %all-to-all-start = ((bf16[4,208,364]{2,1,0:T(8,128)(2,1)}), bf16[4,208,364]{2,1,0:T(8,128)(2,1)S(1)}, u32[]{:S(2)}, u32[]{:S(2)}) async-start(bf16[4,208,364]{2,1,0:T(8,128)(2,1)} %select_select_fusion.1), calls=%async_computation | async-start | bytes 1277952 | tf_op jit(solution)/shard_map/all_to_all | solution.py:64
  34.3 8.5 %copy-start.2 = (s32[56,28]{0,1:T(8,128)S(1)}, s32[56,28]{0,1:T(8,128)}, u32[]{:S(2)}) copy-start(s32[56,28]{0,1:T(8,128)} %param.5) | copy-start | bytes 18820
  35.3 24.2 %all-to-all-start.1 = ((bf16[728,8,52]{0,2,1:T(8,128)(2,1)}), bf16[728,8,52]{0,2,1:T(8,128)(2,1)S(1)}, u32[]{:S(2)}, u32[]{:S(2)}) async-start(bf16[728,8,52]{0,2,1:T(8,128)(2,1)} %select_select_fusion), calls=%async_computation.1 | async-start | bytes 1376256 | tf_op jit(solution)/shard_map/all_to_all | solution.py:72
  41.9 138.0 %all-gather.12.cloned.1.call-start = ((), (), s32[]{:S(2)}) async-start(), calls=%async_computation.5 | async-start | bytes 5031936 | tf_op jit(solution)/shard_map/all_gather | solution.py:83
  103.3 100.0 %all-gather.8.cloned.1.call-start = ((), (), s32[]{:S(2)}) async-start(), calls=%async_computation.3 | async-start | bytes 2795520 | tf_op jit(solution)/shard_map/all_gather | solution.py:37
  104.1 177.7 %all-gather.6.cloned.1.call-start = ((), (), s32[]{:S(2)}) async-start(), calls=%async_computation.2 | async-start | bytes 5031936 | tf_op jit(solution)/shard_map/all_gather | solution.py:85
  114.6 190.4 %all-gather.10.cloned.1.call-start = ((), (), s32[]{:S(2)}) async-start(), calls=%async_computation.4 | async-start | bytes 2795520 | tf_op jit(solution)/shard_map/all_gather | solution.py:37
  286.7 18.3 %copy-start.1 = (bf16[728,364]{1,0:T(8,128)(2,1)S(1)}, bf16[728,364]{1,0:T(8,128)(2,1)}, u32[]{:S(2)}) copy-start(bf16[728,364]{1,0:T(8,128)(2,1)} %multiply_convert_fusion.1) | copy-start | bytes 1589956
Sparse Core Ops, SparseCore 0:
  103.4 76.4 all-gather.11
  181.5 21.7 all-gather.7
  205.5 76.2 all-gather.5
  283.2 21.7 all-gather.9
